TPU v7x, 32 devices: a whole 2x2x4 slice. The times are simulated.
32 devices in a mesh: seq: 8 (over z, y), grp: 4 (over x, core).
Axes of the slice: x: 2, y: 2, z: 4, core: 2. Of those that a mesh axis runs over, the one named last changes fastest.
Arguments:
- frames: bfloat16 [16384, 1024], P(('seq', 'grp')), may hold values from -6 to 6
- ln1_gain: float32 [1024], replicated, may hold values from 0.1 to 1.9
- w_in: bfloat16 [1024, 2, 1024], P('seq', None, 'grp'), may hold values from -0.1875 to 0.1875
- w_dw: bfloat16 [31, 1024], replicated, may hold values from -1 to 1
- ln2_gain: float32 [1024], replicated, may hold values from 0.1 to 1.9
- ln2_bias: float32 [1024], replicated, may hold values from -3 to 3
- w_out: bfloat16 [1024, 1024], P('grp', 'seq'), may hold values from -0.1875 to 0.1875
- block_utt: int32 [128], replicated, may hold values from 0 to 31, as said below
- block_off: int32 [128], replicated, may hold values from 0 to 6, as said below
- lengths: int32 [32], replicated, may hold values from 1 to 896, as said below
Outputs:
- result: bfloat16 [16384, 1024], P(('seq', 'grp'))
Inputs may be any that keep to these rules, and one draw needn't show every extreme that they name: block_utt never falls along the blocks and names every utterance; each utterance is one run of 1 to 7 whole blocks, and some utterance has exactly 7. block_off counts the blocks of the run before a block, starting at 0. `lengths`: an utterance of n blocks has more than (n - 1) * 128 and at most n * 128 live frames.
All inputs are finite; a program needn't handle non-finite values.
Results may differ from a plain program's by a relative error of at most 0.0046.
Values may be sent and summed in bfloat16 or wider, within the bound.
A program may use at most 64 MiB of HBM per device.

v0:
```python
import jax
import jax.numpy as jnp
from jax import lax
from jax.sharding import PartitionSpec as P

D = 1024
KER = 31
BLK = 128
epsilon = 1e-05


def extended(block, sides, width):
    for axis, dim in sides:
        count = lax.axis_size(axis)
        forward = [(i, i + 1) for i in range(count - 1)]
        backward = [(target, source) for source, target in forward]
        low = lax.ppermute(
            lax.slice_in_dim(block, block.shape[dim] - width, None, axis=dim), axis, forward
        )
        high = lax.ppermute(lax.slice_in_dim(block, 0, width, axis=dim), axis, backward)
        block = jnp.concatenate([low, block, high], axis=dim)
    return block


def frame_keys(block_utt, block_off, lengths, first_row, row_count, margin):
    places = first_row - margin + jnp.arange(row_count + 2 * margin, dtype=jnp.int32)
    total_rows = block_utt.shape[0] * BLK
    inside = (places >= 0) & (places < total_rows)
    blocks = jnp.clip(places // BLK, 0, block_utt.shape[0] - 1)
    utterance = jnp.take(block_utt, blocks)
    position = jnp.take(block_off, blocks) * BLK + places % BLK
    living = inside & (position < jnp.take(lengths, utterance))
    return (jnp.where(living, utterance, -1), living[margin : margin + row_count])


def layer_norm(rows, gain):
    values = rows.astype(jnp.float32)
    average = jnp.mean(values, axis=1, keepdims=True)
    centered = values - average
    spread = jnp.mean(centered * centered, axis=1, keepdims=True)
    return (centered * lax.rsqrt(spread + epsilon) * gain).astype(jnp.bfloat16)


def gate_units(projected, living):
    half = projected.shape[1] // 2
    values = projected[:, :half] * jax.nn.sigmoid(projected[:, half:])
    return (values * living.astype(jnp.float32)[:, None]).astype(jnp.bfloat16)


def depthwise(widened, keys_wide, taps, row_count):
    margin = (taps.shape[0] - 1) // 2
    center = keys_wide[margin : margin + row_count]
    summed = jnp.zeros((row_count, widened.shape[1]), jnp.float32)
    for tap_index in range(taps.shape[0]):
        shifted = widened[tap_index : tap_index + row_count].astype(jnp.float32)
        same = (keys_wide[tap_index : tap_index + row_count] == center)[:, None]
        summed = summed + jnp.where(same, shifted, 0.0) * taps[tap_index].astype(jnp.float32)
    return summed


def finish(mixed, stat_sum, square_sum, width_total, gain, bias):
    average = stat_sum / width_total
    spread = square_sum / width_total - average * average
    normed = (mixed - average[:, None]) * lax.rsqrt(spread + epsilon)[:, None] * gain + bias
    return (normed * jax.nn.sigmoid(normed)).astype(jnp.bfloat16)


def project_rows(normed, row_count, column_count):

    def add_rows(total, weight_piece, start_row):
        piece_rows = weight_piece.shape[0]
        return jnp.dot(
            normed, weight_piece.reshape(piece_rows, -1), preferred_element_type=jnp.float32
        )

    return (add_rows, jnp.zeros((row_count, column_count), jnp.float32))


def per_device(
    frames, ln1_gain, w_in, w_dw, ln2_gain, ln2_bias, w_out, block_utt, block_off, lengths
):
    row_count = frames.shape[0]
    margin = (KER - 1) // 2
    own_first = lax.axis_index(("seq", "grp")) * row_count
    keys_wide, living = frame_keys(block_utt, block_off, lengths, own_first, row_count, margin)
    normed = layer_norm(frames, ln1_gain)
    w_in_rows, w_out_rows = (
        lax.all_gather(w_in, "grp", axis=2, tiled=True),
        lax.all_gather(w_out, "grp", axis=0, tiled=True),
    )
    add_rows, empty = project_rows(normed, row_count, 2 * D)
    projected = add_rows(empty, lax.all_gather(w_in_rows, "seq", axis=0, tiled=True), jnp.int32(0))
    gated = gate_units(projected, living)
    widened = extended(gated, ((("seq", "grp"), 0),), margin)
    mixed = depthwise(widened, keys_wide, w_dw, row_count)
    act = finish(
        mixed, jnp.sum(mixed, axis=1), jnp.sum(mixed * mixed, axis=1), float(D), ln2_gain, ln2_bias
    )
    output = jnp.dot(
        act,
        lax.all_gather(w_out_rows, "seq", axis=1, tiled=True),
        preferred_element_type=jnp.float32,
    )
    alive = living.astype(jnp.float32)[:, None]
    return (frames.astype(jnp.float32) + output * alive).astype(jnp.bfloat16)


def solution(mesh):
    return jax.shard_map(
        per_device,
        mesh=mesh,
        in_specs=(
            P(("seq", "grp"), None),
            P(),
            P("seq", None, "grp"),
            P(),
            P(),
            P(),
            P("grp", "seq"),
            P(),
            P(),
            P(),
        ),
        out_specs=P(("seq", "grp"), None),
        check_vma=False,
    )
```

profile of v0, /device:TPU:0, one launch (start us, length us, event | category | flops | bytes accessed | tf_op | source)
XLA Modules:
  0.0 152.2 jit_solution(5140980709808963621)
XLA Ops:
  6.5 10.5 %all_gather.12 = bf16[128,2,1024]{2,1,0:T(2,128)(2,1)} all-gather(bf16[128,2,256]{2,1,0:T(2,128)(2,1)} %param.14), channel_id=1, replica_groups=mesh['seq'=8,'grp'=4] {'grp'}, dimensions={2}, use_global_device_ids=true | all-gather | bytes 655360 | tf_op jit(solution)/shard_map/all_gather | solution.py:88
  17.1 6.5 %all_gather.14 = bf16[1024,128]{1,0:T(8,128)(2,1)} all-gather(bf16[256,128]{1,0:T(8,128)(2,1)} %param.18), channel_id=1, replica_groups=mesh['seq'=8,'grp'=4] {'grp'}, dimensions={0}, use_global_device_ids=true | all-gather | bytes 327680 | tf_op jit(solution)/shard_map/all_gather | solution.py:89
  23.6 2.1 %fusion.67 = (s32[1]{0:T(128)}, s32[1]{0:T(128)}, s32[1]{0:T(128)}, s32[1]{0:T(128)}, s32[1]{0:T(128)}, /*index=5*/s32[1]{0:T(128)}, s32[1]{0:T(128)}, s32[1]{0:...) fusion(s32[32]{0:T(128)} %param.21), kind=kLoop, calls=%fused_computation.200 | loop fusion | bytes 152 | tf_op jit(solution)/shard_map/jit(_take)/gather | solution.py:32
  25.7 1.8 %fusion.68 = (s32[1]{0:T(128)}, s32[1]{0:T(128)}, s32[1]{0:T(128)}, s32[1]{0:T(128)}, s32[1]{0:T(128)}, /*index=5*/s32[1]{0:T(128)}, s32[1]{0:T(128)}, s32[1]{0:...) fusion(s32[32]{0:T(128)} %param.21), kind=kLoop, calls=%fused_computation.201 | loop fusion | bytes 104 | tf_op jit(solution)/shard_map/jit(_take)/gather | solution.py:32
  27.6 3.8 %gather_fusion = s32[542]{0:T(1024)S(1)} fusion(s32[128]{0:T(128)S(1)} %copy-done, s32[1024]{0:T(1024)S(1)} %pad_clamp_fusion), kind=kCustom, calls=%fused_computation.clone | custom fusion | bytes 6504 | tf_op jit(solution)/shard_map/jit(_take)/gather | solution.py:31
  31.4 3.8 %gather_fusion.1 = s32[542]{0:T(1024)S(1)} fusion(s32[128]{0:T(128)S(1)} %copy-done.1, s32[1024]{0:T(1024)S(1)} %pad_clamp_fusion), kind=kCustom, calls=%fused_computation.1.clone | custom fusion | bytes 6504 | tf_op jit(solution)/shard_map/jit(_take)/gather | solution.py:30
  35.3 20.1 %fusion.62 = (s32[542]{0:T(1024)S(1)}, pred[542]{0:T(1024)(128)(4,1)S(1)}) fusion(s32[542]{0:T(1024)S(1)} %gather_fusion.1, s32[]{:T(128)S(6)} %sub.32, s32[]{:T(128)} %bitcast.31, s32[]{:T(128)} %bitcast.30, s32[]{:T(128)} %bitcast.29, s32[]{:T(128)} %bitcast.28, s32[]{:T(128)} %bitcast.27, s32[]{:T(128)} %bitcast.26, s32[]{:T(128)} %bitcast.25, ...), kind=kLoop, calls=%fused_computation.161 | loop fusion | flops 57452 | bytes 7178 | tf_op jit(solution)/shard_map/jit(_where)/select_n | solution.py:33
  55.4 0.1 slice_compare_fusion.29
  55.5 0.1 slice_compare_fusion.28
  55.6 0.1 slice_compare_fusion.27
  55.8 0.1 slice_convert_fusion.31
  55.9 0.2 convert_reduce_fusion
  56.1 0.4 fusion.2
  56.5 33.8 %all-gather.3.cloned.1.call-done = bf16[1024,2,1024]{2,1,0:T(2,128)(2,1)} async-done(((bf16[128,2,1024]{2,1,0:T(2,128)(2,1)}), bf16[1024,2,1024]{2,1,0:T(2,128)(2,1)}) %all-gather.3.cloned.1.call-update) | async-done | bytes 4194320 | tf_op jit(solution)/shard_map/all_gather | solution.py:92
  90.3 3.6 %copy.11 = bf16[128,8,2,1024]{3,1,2,0:T(8,128)(2,1)S(1)} copy(bf16[128,8,2,1024]{3,2,1,0:T(2,128)(2,1)} %bitcast.67) | data formatting | bytes 8388608
  94.0 2.5 %fusion.12 = f32[512,2048]{1,0:T(8,128)S(1)} fusion(bf16[1024,2048]{1,0:T(8,128)(2,1)S(1)} %bitcast.68, bf16[512,1024]{1,0:T(8,128)(2,1)S(1)} %copy-done.2, f32[1024]{0:T(1024)S(1)} %copy-done.4, f32[512]{0:T(512)S(1)} %add_rsqrt_fusion.1, f32[512]{0:T(512)S(1)} %broadcast_multiply_fusion.1), kind=kOutput, calls=%fused_computation.49 | convolution fusion | flops 2150105088 | bytes 9445376 | tf_op jit(solution)/shard_map/dot_general | solution.py:72
  96.5 0.6 fusion.11
  97.1 1.3 collective-permute-start
  98.4 1.5 collective-permute-start.1
  99.9 0.1 slice_compare_fusion.26
  99.9 3.3 %collective-permute-done.1 = bf16[15,1024]{1,0:T(8,128)(2,1)S(1)} collective-permute-done((bf16[15,1024]{1,0:T(8,128)(2,1)S(1)}, bf16[15,1024]{1,0:T(8,128)(2,1)S(1)}, u32[]{:S(2)}, u32[]{:S(2)}) %collective-permute-start.1) | collective-permute-done | bytes 30752 | tf_op jit(solution)/shard_map/ppermute | solution.py:20
  103.2 19.4 %fusion.64 = (f32[512]{0:T(512)S(1)}, f32[512]{0:T(512)S(1)}, f32[512,1024]{1,0:T(8,128)S(1)}) fusion(f32[1024]{0:T(1024)S(1)} %bitcast.98, bf16[15,1024]{1,0:T(8,128)(2,1)S(1)} %collective-permute-done.1, bf16[512,1024]{1,0:T(8,128)(2,1)S(1)} %fusion.11, pred[512]{0:T(512)(128)(4,1)S(1)} %get-tuple-element.73, f32[1024]{0:T(1024)S(1)} %bitcast.99, ...), kind=kLoop, calls=%fused_computation.198 | loop fusion | flops 112720896 | bytes 3353600 | tf_op jit(solution)/shard_map/reduce_sum | solution.py:97
  122.6 18.7 %all-gather.5.cloned.1.call-done = bf16[1024,1024]{1,0:T(8,128)(2,1)} async-done(((bf16[1024,128]{1,0:T(8,128)(2,1)}), bf16[1024,1024]{1,0:T(8,128)(2,1)}) %all-gather.5.cloned.1.call-update) | async-done | bytes 2097168 | tf_op jit(solution)/shard_map/all_gather | solution.py:101
  141.3 4.1 %fusion.5 = bf16[512,1024]{1,0:T(8,128)(2,1)} fusion(bf16[512,1024]{1,0:T(8,128)(2,1)S(1)} %copy-done.2, bf16[1024,1024]{1,0:T(8,128)(2,1)} %all-gather.5.cloned.1.call-done, f32[512,1024]{1,0:T(8,128)S(1)} %get-tuple-element.8, f32[1024]{0:T(1024)S(1)} %copy-done.5, f32[1024]{0:T(1024)S(1)} %copy-done.6, f32[512]{0:T(512)S(1)} %get-tuple-element.75, ...), kind=kOutput, calls=%fused_computation.38 | convolution fusion | flops 1080557568 | bytes 6305792 | tf_op jit(solution)/shard_map/dot_general | solution.py:99
  (27 shorter events, 0.3 us)
Async XLA Ops:
  6.5 21.1 %copy-start = (s32[128]{0:T(128)S(1)}, s32[128]{0:T(128)}, u32[]{:S(2)}) copy-start(s32[128]{0:T(128)} %param.20) | copy-start | bytes 1540
  6.5 83.8 %all-gather.3.cloned.1.call-start = ((), (), s32[]{:S(2)}) async-start(), calls=%async_computation | async-start | bytes 4718592 | tf_op jit(solution)/shard_map/all_gather | solution.py:92
  17.0 124.3 %all-gather.5.cloned.1.call-start = ((), (), s32[]{:S(2)}) async-start(), calls=%async_computation.1 | async-start | bytes 2359296 | tf_op jit(solution)/shard_map/all_gather | solution.py:101
  27.6 3.8 %copy-start.1 = (s32[128]{0:T(128)S(1)}, s32[128]{0:T(128)}, u32[]{:S(2)}) copy-start(s32[128]{0:T(128)} %param.19) | copy-start | bytes 1540
  31.4 24.2 %copy-start.3 = (bf16[31,1024]{1,0:T(8,128)(2,1)S(1)}, bf16[31,1024]{1,0:T(8,128)(2,1)}, u32[]{:S(2)}) copy-start(bf16[31,1024]{1,0:T(8,128)(2,1)} %param.15) | copy-start | bytes 190468
  31.4 24.4 %copy-start.2 = (bf16[512,1024]{1,0:T(8,128)(2,1)S(1)}, bf16[512,1024]{1,0:T(8,128)(2,1)}, u32[]{:S(2)}) copy-start(bf16[512,1024]{1,0:T(8,128)(2,1)} %param.12) | copy-start | bytes 3145732
  90.3 3.6 %copy-start.4 = (f32[1024]{0:T(1024)S(1)}, f32[1024]{0:T(1024)}, u32[]{:S(2)}) copy-start(f32[1024]{0:T(1024)} %param.13) | copy-start | bytes 12292
  97.0 44.3 %copy-start.5 = (f32[1024]{0:T(1024)S(1)}, f32[1024]{0:T(1024)}, u32[]{:S(2)}) copy-start(f32[1024]{0:T(1024)} %param.17) | copy-start | bytes 12292
  97.1 44.3 %copy-start.6 = (f32[1024]{0:T(1024)S(1)}, f32[1024]{0:T(1024)}, u32[]{:S(2)}) copy-start(f32[1024]{0:T(1024)} %param.16) | copy-start | bytes 12292
  97.1 2.9 %collective-permute-start = (bf16[15,1024]{1,0:T(8,128)(2,1)S(1)}, bf16[15,1024]{1,0:T(8,128)(2,1)S(1)}, u32[]{:S(2)}, u32[]{:S(2)}) collective-permute-start(bf16[15,1024]{1,0:T(8,128)(2,1)S(1)} %get-tuple-element.11), channel_id=1, source_target_pairs={{0,1},{1,2},{2,3},{3,4},{4,5},{5,6},{6,7},{7,8},{8,9},{9,10},{10,1... | collective-permute-start | bytes 92168 | tf_op jit(solution)/shard_map/ppermute | solution.py:17
  98.4 4.9 %collective-permute-start.1 = (bf16[15,1024]{1,0:T(8,128)(2,1)S(1)}, bf16[15,1024]{1,0:T(8,128)(2,1)S(1)}, u32[]{:S(2)}, u32[]{:S(2)}) collective-permute-start(bf16[15,1024]{1,0:T(8,128)(2,1)S(1)} %get-tuple-element.12), channel_id=1, source_target_pairs={{1,0},{2,1},{3,2},{4,3},{5,4},{6,5},{7,6},{8,7},{9,8},{10,9},{11,1... | collective-permute-start | bytes 92168 | tf_op jit(solution)/shard_map/ppermute | solution.py:20
Sparse Core Ops, SparseCore 0:
  17.2 73.1 all-gather.2
  92.4 48.8 all-gather.4
where the time goes:
time: 153 us; the launch traced here: 152 us
  waiting for transfers between devices  55.8 us (36%)
  other arithmetic  41.3 us (27%)
  blocking collectives  17 us (11%)
  local copies, waits for them, and re-layouts  15.2 us (10%)
  between operations  13.6 us (9%)
  matrix products  6.55 us (4%)
  starting transfers between devices  2.81 us (2%)
    all_gather x1, waiting for transfers between devices, per_device(): lax.all_gather(w_in_rows, 'seq', axis=0, tiled=True)  33.8 us
    select_n x1, other arithmetic, frame_keys(): return (jnp.where(living, utterance, -1), living[margin:margin + row_count])  20.1 us
    reduce_sum x1, other arithmetic, per_device(): jnp.sum(mixed, axis=1)  19.4 us
    all_gather x1, waiting for transfers between devices, per_device(): lax.all_gather(w_out_rows, 'seq', axis=1, tiled=True)  18.7 us
    all_gather x1, blocking collectives, per_device(): lax.all_gather(w_in, 'grp', axis=2, tiled=True)  10.5 us
    all_gather x1, blocking collectives, per_device(): lax.all_gather(w_out, 'grp', axis=0, tiled=True)  6.53 us
    dot_general x1, matrix products, per_device(): jnp.dot(act, lax.all_gather(w_out_rows, 'seq', axis=1, tiled=True), prefe...  4.06 us
    gather x2, local copies, waits for them, and re-layouts, frame_keys(): living = inside & (position < jnp.take(lengths, utterance))  3.9 us
  transfers between devices with their start and end apart: 4, of which 3 were waited for; matrix products, arithmetic and copies ran while one was open for 39% of the time, Pallas kernels for 0%

commit v1 on v0

--- a/solution.py
+++ b/solution.py
@@ -2,11 +2,17 @@
 import jax.numpy as jnp
 from jax import lax
 from jax.sharding import PartitionSpec as P
+from jax.lax import all_gather
 
 D = 1024
 KER = 31
 BLK = 128
 epsilon = 1e-05
+
+
+def _meet_task(vec):
+    view_out = jnp.concatenate(all_gather(vec, "grp"), axis=2)
+    return view_out
 
 
 def extended(block, sides, width):
@@ -84,10 +90,7 @@
     own_first = lax.axis_index(("seq", "grp")) * row_count
     keys_wide, living = frame_keys(block_utt, block_off, lengths, own_first, row_count, margin)
     normed = layer_norm(frames, ln1_gain)
-    w_in_rows, w_out_rows = (
-        lax.all_gather(w_in, "grp", axis=2, tiled=True),
-        lax.all_gather(w_out, "grp", axis=0, tiled=True),
-    )
+    w_in_rows, w_out_rows = (_meet_task(w_in), lax.all_gather(w_out, "grp", axis=0, tiled=True))
     add_rows, empty = project_rows(normed, row_count, 2 * D)
     projected = add_rows(empty, lax.all_gather(w_in_rows, "seq", axis=0, tiled=True), jnp.int32(0))
     gated = gate_units(projected, living)

time: 153 us -> 155 us (1.013)
  waiting for transfers between devices: 55.8 us -> 62.2 us
  local copies, waits for them, and re-layouts: 15.2 us -> 11 us
  matrix products: 6.55 us -> 8.67 us
  blocking collectives: 17 us -> 15 us
    all_gather x1, waiting for transfers between devices: 33.8 us -> 38.9 us  [per_device(): lax.all_gather(w_in_rows, 'seq', axis=0, tiled=True)]
    unnamed x15 -> x19, local copies, waits for them, and re-layouts: 3.67 us -> 1 us
    gather x2, local copies, waits for them, and re-layouts: 3.9 us -> 1.42 us  [frame_keys(): living = inside & (position < jnp.take(lengths, utterance))]
    dot_general x1, matrix products: 2.49 us -> 4.61 us  [add_rows(): jnp.dot(normed, weight_piece.reshape(piece_rows, -1), preferred_element_t...]
    all_gather x1, blocking collectives: 10.5 us -> 8.65 us  [_meet_task(): view_out = jnp.concatenate(all_gather(vec, 'grp'), axis=2)]
  transfers between devices with their start and end apart: 4 -> 4, of which waited for: 3 -> 3; matrix products, arithmetic and copies ran while one was open for 39% -> 36% of each run, Pallas kernels for 0% -> 0%
where the time goes in v1:
time: 155 us; the launch traced here: 154 us
  waiting for transfers between devices  62.2 us (40%)
  other arithmetic  41.2 us (27%)
  blocking collectives  15 us (10%)
  between operations  13.6 us (9%)
  local copies, waits for them, and re-layouts  11 us (7%)
  matrix products  8.67 us (6%)
  starting transfers between devices  2.81 us (2%)
    all_gather x1, waiting for transfers between devices, per_device(): lax.all_gather(w_in_rows, 'seq', axis=0, tiled=True)  38.9 us
    select_n x1, other arithmetic, frame_keys(): return (jnp.where(living, utterance, -1), living[margin:margin + row_count])  20.1 us
    all_gather x1, waiting for transfers between devices, per_device(): lax.all_gather(w_out_rows, 'seq', axis=1, tiled=True)  19.9 us
    reduce_sum x1, other arithmetic, per_device(): jnp.sum(mixed, axis=1)  19.4 us
    all_gather x1, blocking collectives, _meet_task(): view_out = jnp.concatenate(all_gather(vec, 'grp'), axis=2)  8.65 us
    all_gather x1, blocking collectives, per_device(): lax.all_gather(w_out, 'grp', axis=0, tiled=True)  6.3 us
    dot_general x1, matrix products, add_rows(): jnp.dot(normed, weight_piece.reshape(piece_rows, -1), preferred_element_t...  4.61 us
    dot_general x1, matrix products, per_device(): jnp.dot(act, lax.all_gather(w_out_rows, 'seq', axis=1, tiled=True), prefe...  4.06 us
  transfers between devices with their start and end apart: 4, of which 3 were waited for; matrix products, arithmetic and copies ran while one was open for 36% of the time, Pallas kernels for 0%

profile of v1, /device:TPU:0, one launch (start us, length us, event | category | flops | bytes accessed | tf_op | source)
XLA Modules:
  0.0 154.4 jit_solution(8378934198657159494)
XLA Ops:
  6.5 1.0 copy.11
  7.5 8.6 %all-gather = bf16[512,2,256]{2,0,1:T(8,128)(2,1)S(1)} all-gather(bf16[128,2,256]{2,0,1:T(8,128)(2,1)S(1)} %copy.11), channel_id=2, replica_groups=mesh['seq'=8,'grp'=4] {'grp'}, dimensions={0}, use_global_device_ids=true | all-gather | bytes 655360 | tf_op jit(solution)/shard_map/all_gather | solution.py:14
  16.2 1.0 copy.12
  17.2 6.3 %all_gather.18 = bf16[1024,128]{1,0:T(8,128)(2,1)} all-gather(bf16[256,128]{1,0:T(8,128)(2,1)S(1)} %copy-done.5), channel_id=1, replica_groups=mesh['seq'=8,'grp'=4] {'grp'}, dimensions={0}, use_global_device_ids=true | all-gather | bytes 327680 | tf_op jit(solution)/shard_map/all_gather | solution.py:93
  23.6 0.7 fusion.67
  24.3 0.7 fusion.68
  25.1 3.8 %gather_fusion = s32[542]{0:T(1024)S(1)} fusion(s32[128]{0:T(128)S(1)} %copy-done, s32[1024]{0:T(1024)S(1)} %pad_clamp_fusion), kind=kCustom, calls=%fused_computation.clone | custom fusion | bytes 6504 | tf_op jit(solution)/shard_map/jit(_take)/gather | solution.py:37
  28.9 3.8 %gather_fusion.1 = s32[542]{0:T(1024)S(1)} fusion(s32[128]{0:T(128)S(1)} %copy-done.1, s32[1024]{0:T(1024)S(1)} %pad_clamp_fusion), kind=kCustom, calls=%fused_computation.1.clone | custom fusion | bytes 6504 | tf_op jit(solution)/shard_map/jit(_take)/gather | solution.py:36
  32.7 20.1 %fusion.62 = (s32[542]{0:T(1024)S(1)}, pred[542]{0:T(1024)(128)(4,1)S(1)}) fusion(s32[542]{0:T(1024)S(1)} %gather_fusion.1, s32[]{:T(128)S(6)} %sub.32, s32[]{:T(128)} %bitcast.31, s32[]{:T(128)} %bitcast.30, s32[]{:T(128)} %bitcast.29, s32[]{:T(128)} %bitcast.28, s32[]{:T(128)} %bitcast.27, s32[]{:T(128)} %bitcast.26, s32[]{:T(128)} %bitcast.25, ...), kind=kLoop, calls=%fused_computation.161 | loop fusion | flops 57452 | bytes 7178 | tf_op jit(solution)/shard_map/jit(_where)/select_n | solution.py:39
  52.8 0.1 slice_compare_fusion.29
  52.9 0.1 slice_compare_fusion.28
  53.0 0.1 slice_compare_fusion.27
  53.2 0.2 convert_reduce_fusion
  53.5 0.4 fusion.2
  53.9 38.9 %all-gather.4.cloned.1.call-done = bf16[1024,2,1024]{0,2,1:T(8,128)(2,1)} async-done(((bf16[128,2,1024]{0,2,1:T(8,128)(2,1)}), bf16[1024,2,1024]{0,2,1:T(8,128)(2,1)}) %all-gather.4.cloned.1.call-update) | async-done | bytes 4194320 | tf_op jit(solution)/shard_map/all_gather | solution.py:95
  92.8 4.6 %fusion.12 = f32[512,2048]{1,0:T(8,128)S(1)} fusion(bf16[1024,2048]{0,1:T(8,128)(2,1)} %bitcast.103, bf16[512,1024]{1,0:T(8,128)(2,1)S(1)} %copy-done.2, f32[1024]{0:T(1024)S(1)} %copy-done.6, f32[512]{0:T(512)S(1)} %add_rsqrt_fusion.1, f32[512]{0:T(512)S(1)} %broadcast_multiply_fusion.1), kind=kOutput, calls=%fused_computation.49 | convolution fusion | flops 2150105088 | bytes 9445376 | tf_op jit(solution)/shard_map/dot_general | solution.py:78
  97.4 0.6 fusion.11
  98.0 1.3 collective-permute-start
  99.3 1.5 collective-permute-start.1
  100.8 0.1 slice_compare_fusion.26
  100.9 3.3 %collective-permute-done.1 = bf16[15,1024]{1,0:T(8,128)(2,1)S(1)} collective-permute-done((bf16[15,1024]{1,0:T(8,128)(2,1)S(1)}, bf16[15,1024]{1,0:T(8,128)(2,1)S(1)}, u32[]{:S(2)}, u32[]{:S(2)}) %collective-permute-start.1) | collective-permute-done | bytes 30752 | tf_op jit(solution)/shard_map/ppermute | solution.py:26
  104.2 19.4 %fusion.64 = (f32[512]{0:T(512)S(1)}, f32[512]{0:T(512)S(1)}, f32[512,1024]{1,0:T(8,128)S(1)}) fusion(f32[1024]{0:T(1024)S(1)} %bitcast.101, bf16[15,1024]{1,0:T(8,128)(2,1)S(1)} %collective-permute-done.1, bf16[512,1024]{1,0:T(8,128)(2,1)S(1)} %fusion.11, pred[512]{0:T(512)(128)(4,1)S(1)} %get-tuple-element.73, f32[1024]{0:T(1024)S(1)} %bitcast.102, ...), kind=kLoop, calls=%fused_computation.198 | loop fusion | flops 112720896 | bytes 3353600 | tf_op jit(solution)/shard_map/reduce_sum | solution.py:100
  123.6 19.9 %all-gather.6.cloned.1.call-done = bf16[1024,1024]{1,0:T(8,128)(2,1)} async-done(((bf16[1024,128]{1,0:T(8,128)(2,1)}), bf16[1024,1024]{1,0:T(8,128)(2,1)}) %all-gather.6.cloned.1.call-update) | async-done | bytes 2097168 | tf_op jit(solution)/shard_map/all_gather | solution.py:104
  143.5 4.1 %fusion.5 = bf16[512,1024]{1,0:T(8,128)(2,1)} fusion(bf16[512,1024]{1,0:T(8,128)(2,1)S(1)} %copy-done.2, bf16[1024,1024]{1,0:T(8,128)(2,1)} %all-gather.6.cloned.1.call-done, f32[512,1024]{1,0:T(8,128)S(1)} %get-tuple-element.8, f32[1024]{0:T(1024)S(1)} %copy-done.7, f32[1024]{0:T(1024)S(1)} %copy-done.8, f32[512]{0:T(512)S(1)} %get-tuple-element.75, ...), kind=kOutput, calls=%fused_computation.38 | convolution fusion | flops 1080557568 | bytes 6305792 | tf_op jit(solution)/shard_map/dot_general | solution.py:102
  (32 shorter events, 0.4 us)
Async XLA Ops:
  6.5 18.5 %copy-start = (s32[128]{0:T(128)S(1)}, s32[128]{0:T(128)}, u32[]{:S(2)}) copy-start(s32[128]{0:T(128)} %param.20) | copy-start | bytes 1540
  6.5 10.7 %copy-start.5 = (bf16[256,128]{1,0:T(8,128)(2,1)S(1)}, bf16[256,128]{1,0:T(8,128)(2,1)}, u32[]{:S(2)}) copy-start(bf16[256,128]{1,0:T(8,128)(2,1)} %param.18) | copy-start | bytes 196612
  6.5 17.0 %copy-start.3 = (s32[32]{0:T(128)S(1)}, s32[32]{0:T(128)}, u32[]{:S(2)}) copy-start(s32[32]{0:T(128)} %param.21) | copy-start | bytes 388
  6.5 86.3 %all-gather.4.cloned.1.call-start = ((), (), s32[]{:S(2)}) async-start(), calls=%async_computation | async-start | bytes 4718592 | tf_op jit(solution)/shard_map/all_gather | solution.py:95
  17.2 126.4 %all-gather.6.cloned.1.call-start = ((), (), s32[]{:S(2)}) async-start(), calls=%async_computation.1 | async-start | bytes 2359296 | tf_op jit(solution)/shard_map/all_gather | solution.py:104
  25.0 3.8 %copy-start.1 = (s32[128]{0:T(128)S(1)}, s32[128]{0:T(128)}, u32[]{:S(2)}) copy-start(s32[128]{0:T(128)} %param.19) | copy-start | bytes 1540
  28.9 24.2 %copy-start.4 = (bf16[31,1024]{1,0:T(8,128)(2,1)S(1)}, bf16[31,1024]{1,0:T(8,128)(2,1)}, u32[]{:S(2)}) copy-start(bf16[31,1024]{1,0:T(8,128)(2,1)} %param.15) | copy-start | bytes 190468
  28.9 24.4 %copy-start.2 = (bf16[512,1024]{1,0:T(8,128)(2,1)S(1)}, bf16[512,1024]{1,0:T(8,128)(2,1)}, u32[]{:S(2)}) copy-start(bf16[512,1024]{1,0:T(8,128)(2,1)} %param.12) | copy-start | bytes 3145732
  32.7 60.1 %copy-start.6 = (f32[1024]{0:T(1024)S(1)}, f32[1024]{0:T(1024)}, u32[]{:S(2)}) copy-start(f32[1024]{0:T(1024)} %param.13) | copy-start | bytes 12292
  98.0 45.5 %copy-start.7 = (f32[1024]{0:T(1024)S(1)}, f32[1024]{0:T(1024)}, u32[]{:S(2)}) copy-start(f32[1024]{0:T(1024)} %param.17) | copy-start | bytes 12292
  98.0 45.5 %copy-start.8 = (f32[1024]{0:T(1024)S(1)}, f32[1024]{0:T(1024)}, u32[]{:S(2)}) copy-start(f32[1024]{0:T(1024)} %param.16) | copy-start | bytes 12292
  98.0 2.9 %collective-permute-start = (bf16[15,1024]{1,0:T(8,128)(2,1)S(1)}, bf16[15,1024]{1,0:T(8,128)(2,1)S(1)}, u32[]{:S(2)}, u32[]{:S(2)}) collective-permute-start(bf16[15,1024]{1,0:T(8,128)(2,1)S(1)} %get-tuple-element.11), channel_id=1, source_target_pairs={{0,1},{1,2},{2,3},{3,4},{4,5},{5,6},{6,7},{7,8},{8,9},{9,10},{10,1... | collective-permute-start | bytes 92168 | tf_op jit(solution)/shard_map/ppermute | solution.py:23
  99.3 4.9 %collective-permute-start.1 = (bf16[15,1024]{1,0:T(8,128)(2,1)S(1)}, bf16[15,1024]{1,0:T(8,128)(2,1)S(1)}, u32[]{:S(2)}, u32[]{:S(2)}) collective-permute-start(bf16[15,1024]{1,0:T(8,128)(2,1)S(1)} %get-tuple-element.12), channel_id=1, source_target_pairs={{1,0},{2,1},{3,2},{4,3},{5,4},{6,5},{7,6},{8,7},{9,8},{10,9},{11,1... | collective-permute-start | bytes 92168 | tf_op jit(solution)/shard_map/ppermute | solution.py:26
Sparse Core Ops, SparseCore 0:
  17.3 75.4 all-gather.3
  94.8 48.6 all-gather.5
